TPU v7x, 128 devices: a whole 4x4x4 slice. The times are simulated.
128 devices in a mesh: data: 1, ctx: 128 (over z, y, x, core).
Axes of the slice: x: 4, y: 4, z: 4, core: 2. Of those that a mesh axis runs over, the one named last changes fastest.
Arguments:
- hidden: bfloat16 [128, 2048], P(('data', 'ctx'))
- seq_lens: int32 [128], P(('data', 'ctx'))
- w_query: bfloat16 [16, 2048, 2048], replicated
- w_key: bfloat16 [16, 2048, 256], replicated
- w_value: bfloat16 [16, 2048, 256], replicated
- w_out: bfloat16 [16, 2048, 2048], replicated
- k_prefix: bfloat16 [16, 65536, 2, 128], P(None, ('data', 'ctx'))
- v_prefix: bfloat16 [16, 65536, 2, 128], P(None, ('data', 'ctx'))
- k_suffix: bfloat16 [16, 128, 32, 2, 128], P(None, ('data', 'ctx'))
- v_suffix: bfloat16 [16, 128, 32, 2, 128], P(None, ('data', 'ctx'))
Outputs:
- output 1: bfloat16 [128, 2048], P(('data', 'ctx'))
- output 2: bfloat16 [16, 128, 32, 2, 128], P(None, ('data', 'ctx'))
- output 3: bfloat16 [16, 128, 32, 2, 128], P(None, ('data', 'ctx'))
All inputs are finite; a program needn't handle non-finite values.
Results may differ from a plain program's by a relative error of at most 0.0135775.
Values are sent between devices in bfloat16 or wider.
A program may use at most 1.25 GiB of HBM per device.

v0:
```python
import jax
import jax.numpy as jnp
from jax import lax
from jax.sharding import PartitionSpec as P


def solution(mesh):
    ctx_size = mesh.shape['ctx']
    home_axes = ('data', 'ctx')
    row_spec = P(home_axes, None)
    lens_spec = P(home_axes)
    whole_spec = P()
    prefix_spec = P(None, home_axes, None, None)
    cache_spec = P(None, home_axes, None, None, None)

    def local_step(hidden, seq_lens, w_query, w_key, w_value, w_out, k_prefix, v_prefix, k_suffix, v_suffix):
        layers = w_query.shape[0]
        kv_heads = k_prefix.shape[2]
        head_dim = k_prefix.shape[3]
        num_heads = w_query.shape[2] // head_dim
        group_size = num_heads // kv_heads
        home_rows = hidden.shape[0]
        slot_count = k_suffix.shape[2]
        score_scale = head_dim ** -0.5
        slot_ids = lax.broadcasted_iota(jnp.int32, (home_rows, slot_count), 1)
        slot_hit = (slot_ids == seq_lens[:, None])[:, :, None, None]
        slot_live = (slot_ids <= seq_lens[:, None])[:, None, None, :]
        k_layers = []
        v_layers = []
        for layer_idx in range(layers):
            queries = jnp.dot(hidden, w_query[layer_idx], preferred_element_type=jnp.float32).astype(jnp.bfloat16).reshape(home_rows, kv_heads, group_size, head_dim)
            k_new = jnp.dot(hidden, w_key[layer_idx], preferred_element_type=jnp.float32).astype(jnp.bfloat16).reshape(home_rows, 1, kv_heads, head_dim)
            v_new = jnp.dot(hidden, w_value[layer_idx], preferred_element_type=jnp.float32).astype(jnp.bfloat16).reshape(home_rows, 1, kv_heads, head_dim)
            k_cache = jnp.where(slot_hit, k_new, k_suffix[layer_idx])
            v_cache = jnp.where(slot_hit, v_new, v_suffix[layer_idx])
            k_layers.append(k_cache)
            v_layers.append(v_cache)
            group_queries = lax.all_gather(queries, 'ctx', axis=0, tiled=True)
            pre_scores = jnp.einsum('bkgd,pkd->bkgp', group_queries, k_prefix[layer_idx], preferred_element_type=jnp.float32) * score_scale
            pre_max = pre_scores.max(axis=-1)
            pre_exp = jnp.exp(pre_scores - pre_max[..., None])
            pre_mass = pre_exp.sum(axis=-1)
            pre_vals = jnp.einsum('bkgp,pkd->bkgd', pre_exp.astype(jnp.bfloat16), v_prefix[layer_idx], preferred_element_type=jnp.float32)
            part_out = (pre_vals / pre_mass[..., None]).astype(jnp.bfloat16)
            part_lse = pre_max + jnp.log(pre_mass)
            home_out = lax.all_to_all(part_out, 'ctx', 0, 0, tiled=True).reshape(ctx_size, home_rows, kv_heads, group_size, head_dim)
            home_lse = lax.all_to_all(part_lse, 'ctx', 0, 0, tiled=True).reshape(ctx_size, home_rows, kv_heads, group_size)
            suf_scores = jnp.einsum('bkgd,bskd->bkgs', queries, k_cache, preferred_element_type=jnp.float32) * score_scale
            suf_scores = jnp.where(slot_live, suf_scores, -jnp.inf)
            suf_max = suf_scores.max(axis=-1)
            suf_exp = jnp.exp(suf_scores - suf_max[..., None])
            suf_mass = suf_exp.sum(axis=-1)
            suf_vals = jnp.einsum('bkgs,bskd->bkgd', suf_exp.astype(jnp.bfloat16), v_cache, preferred_element_type=jnp.float32)
            row_max = jnp.maximum(home_lse.max(axis=0), suf_max)
            part_weight = jnp.exp(home_lse - row_max)
            suf_weight = jnp.exp(suf_max - row_max)
            mass_sum = part_weight.sum(axis=0) + suf_weight * suf_mass
            mixed_sum = (part_weight[..., None] * home_out.astype(jnp.float32)).sum(axis=0) + suf_weight[..., None] * suf_vals
            attended = (mixed_sum / mass_sum[..., None]).astype(jnp.bfloat16).reshape(home_rows, num_heads * head_dim)
            update = jnp.dot(attended, w_out[layer_idx], preferred_element_type=jnp.float32).astype(jnp.bfloat16)
            hidden = (hidden.astype(jnp.float32) + update.astype(jnp.float32)).astype(jnp.bfloat16)
        return hidden, jnp.stack(k_layers), jnp.stack(v_layers)

    return jax.shard_map(local_step, mesh=mesh, in_specs=(row_spec, lens_spec, whole_spec, whole_spec, whole_spec, whole_spec, prefix_spec, prefix_spec, cache_spec, cache_spec), out_specs=(row_spec, cache_spec, cache_spec), check_vma=False)
```

profile of v0, /device:TPU:1, one launch (start us, length us, event | category | flops | bytes accessed | tf_op | source)
XLA Modules:
  0.0 1383.5 jit_solution(2127604415910984681)
XLA Ops:
  11.5 39.2 %all_gather.48 = bf16[128,2,8,128]{3,2,1,0:T(8,128)(2,1)S(1)} all-gather(bf16[1,2,8,128]{3,2,1,0:T(8,128)(2,1)S(1)} %convert_bitcast_fusion.15), channel_id=1, replica_groups=mesh['data'=1,'ctx'=128] {'ctx'}, dimensions={0}, use_global_device_ids=true | all-gather | bytes 528384 | tf_op jit(solution)/shard_map/all_gather | solution.py:38
  116.4 34.5 %all_gather.49 = bf16[128,2,8,128]{3,2,1,0:T(8,128)(2,1)S(1)} all-gather(bf16[1,2,8,128]{3,2,1,0:T(8,128)(2,1)S(1)} %convert_bitcast_fusion.14), channel_id=1, replica_groups=mesh['data'=1,'ctx'=128] {'ctx'}, dimensions={0}, use_global_device_ids=true | all-gather | bytes 528384 | tf_op jit(solution)/shard_map/all_gather | solution.py:38
  205.4 34.5 %all_gather.50 = bf16[128,2,8,128]{3,2,1,0:T(8,128)(2,1)S(1)} all-gather(bf16[1,2,8,128]{3,2,1,0:T(8,128)(2,1)S(1)} %convert_bitcast_fusion.13), channel_id=1, replica_groups=mesh['data'=1,'ctx'=128] {'ctx'}, dimensions={0}, use_global_device_ids=true | all-gather | bytes 528384 | tf_op jit(solution)/shard_map/all_gather | solution.py:38
  295.0 34.5 %all_gather.51 = bf16[128,2,8,128]{3,2,1,0:T(8,128)(2,1)S(1)} all-gather(bf16[1,2,8,128]{3,2,1,0:T(8,128)(2,1)S(1)} %convert_bitcast_fusion.12), channel_id=1, replica_groups=mesh['data'=1,'ctx'=128] {'ctx'}, dimensions={0}, use_global_device_ids=true | all-gather | bytes 528384 | tf_op jit(solution)/shard_map/all_gather | solution.py:38
  381.4 34.5 %all_gather.52 = bf16[128,2,8,128]{3,2,1,0:T(8,128)(2,1)S(1)} all-gather(bf16[1,2,8,128]{3,2,1,0:T(8,128)(2,1)S(1)} %convert_bitcast_fusion.11), channel_id=1, replica_groups=mesh['data'=1,'ctx'=128] {'ctx'}, dimensions={0}, use_global_device_ids=true | all-gather | bytes 528384 | tf_op jit(solution)/shard_map/all_gather | solution.py:38
  439.9 12.8 all-to-all-done.9
  465.4 34.5 %all_gather.53 = bf16[128,2,8,128]{3,2,1,0:T(8,128)(2,1)S(1)} all-gather(bf16[1,2,8,128]{3,2,1,0:T(8,128)(2,1)S(1)} %convert_bitcast_fusion.10), channel_id=1, replica_groups=mesh['data'=1,'ctx'=128] {'ctx'}, dimensions={0}, use_global_device_ids=true | all-gather | bytes 528384 | tf_op jit(solution)/shard_map/all_gather | solution.py:38
  524.1 12.8 all-to-all-done.11
  549.6 34.5 %all_gather.54 = bf16[128,2,8,128]{3,2,1,0:T(8,128)(2,1)S(1)} all-gather(bf16[1,2,8,128]{3,2,1,0:T(8,128)(2,1)S(1)} %convert_bitcast_fusion.9), channel_id=1, replica_groups=mesh['data'=1,'ctx'=128] {'ctx'}, dimensions={0}, use_global_device_ids=true | all-gather | bytes 528384 | tf_op jit(solution)/shard_map/all_gather | solution.py:38
  608.0 12.8 all-to-all-done.13
  633.6 34.5 %all_gather.55 = bf16[128,2,8,128]{3,2,1,0:T(8,128)(2,1)S(1)} all-gather(bf16[1,2,8,128]{3,2,1,0:T(8,128)(2,1)S(1)} %convert_bitcast_fusion.8), channel_id=1, replica_groups=mesh['data'=1,'ctx'=128] {'ctx'}, dimensions={0}, use_global_device_ids=true | all-gather | bytes 528384 | tf_op jit(solution)/shard_map/all_gather | solution.py:38
  692.0 12.8 all-to-all-done.15
  717.6 34.5 %all_gather.56 = bf16[128,2,8,128]{3,2,1,0:T(8,128)(2,1)S(1)} all-gather(bf16[1,2,8,128]{3,2,1,0:T(8,128)(2,1)S(1)} %convert_bitcast_fusion.7), channel_id=1, replica_groups=mesh['data'=1,'ctx'=128] {'ctx'}, dimensions={0}, use_global_device_ids=true | all-gather | bytes 528384 | tf_op jit(solution)/shard_map/all_gather | solution.py:38
  776.2 12.8 all-to-all-done.17
  801.8 34.5 %all_gather.57 = bf16[128,2,8,128]{3,2,1,0:T(8,128)(2,1)S(1)} all-gather(bf16[1,2,8,128]{3,2,1,0:T(8,128)(2,1)S(1)} %convert_bitcast_fusion.6), channel_id=1, replica_groups=mesh['data'=1,'ctx'=128] {'ctx'}, dimensions={0}, use_global_device_ids=true | all-gather | bytes 528384 | tf_op jit(solution)/shard_map/all_gather | solution.py:38
  860.2 12.8 all-to-all-done.19
  885.7 34.5 %all_gather.58 = bf16[128,2,8,128]{3,2,1,0:T(8,128)(2,1)S(1)} all-gather(bf16[1,2,8,128]{3,2,1,0:T(8,128)(2,1)S(1)} %convert_bitcast_fusion.5), channel_id=1, replica_groups=mesh['data'=1,'ctx'=128] {'ctx'}, dimensions={0}, use_global_device_ids=true | all-gather | bytes 528384 | tf_op jit(solution)/shard_map/all_gather | solution.py:38
  944.2 12.8 all-to-all-done.21
  969.7 34.5 %all_gather.59 = bf16[128,2,8,128]{3,2,1,0:T(8,128)(2,1)S(1)} all-gather(bf16[1,2,8,128]{3,2,1,0:T(8,128)(2,1)S(1)} %convert_bitcast_fusion.4), channel_id=1, replica_groups=mesh['data'=1,'ctx'=128] {'ctx'}, dimensions={0}, use_global_device_ids=true | all-gather | bytes 528384 | tf_op jit(solution)/shard_map/all_gather | solution.py:38
  1053.9 34.5 %all_gather.60 = bf16[128,2,8,128]{3,2,1,0:T(8,128)(2,1)S(1)} all-gather(bf16[1,2,8,128]{3,2,1,0:T(8,128)(2,1)S(1)} %convert_bitcast_fusion.3), channel_id=1, replica_groups=mesh['data'=1,'ctx'=128] {'ctx'}, dimensions={0}, use_global_device_ids=true | all-gather | bytes 528384 | tf_op jit(solution)/shard_map/all_gather | solution.py:38
  1138.0 34.5 %all_gather.61 = bf16[128,2,8,128]{3,2,1,0:T(8,128)(2,1)S(1)} all-gather(bf16[1,2,8,128]{3,2,1,0:T(8,128)(2,1)S(1)} %convert_bitcast_fusion.2), channel_id=1, replica_groups=mesh['data'=1,'ctx'=128] {'ctx'}, dimensions={0}, use_global_device_ids=true | all-gather | bytes 528384 | tf_op jit(solution)/shard_map/all_gather | solution.py:38
  1222.0 34.5 %all_gather.62 = bf16[128,2,8,128]{3,2,1,0:T(8,128)(2,1)S(1)} all-gather(bf16[1,2,8,128]{3,2,1,0:T(8,128)(2,1)S(1)} %convert_bitcast_fusion.1), channel_id=1, replica_groups=mesh['data'=1,'ctx'=128] {'ctx'}, dimensions={0}, use_global_device_ids=true | all-gather | bytes 528384 | tf_op jit(solution)/shard_map/all_gather | solution.py:38
  1306.1 34.5 %all_gather.63 = bf16[128,2,8,128]{3,2,1,0:T(8,128)(2,1)S(1)} all-gather(bf16[1,2,8,128]{3,2,1,0:T(8,128)(2,1)S(1)} %convert_bitcast_fusion), channel_id=1, replica_groups=mesh['data'=1,'ctx'=128] {'ctx'}, dimensions={0}, use_global_device_ids=true | all-gather | bytes 528384 | tf_op jit(solution)/shard_map/all_gather | solution.py:38
  1364.4 12.9 all-to-all-done.31
  (568 shorter events, 720.8 us)
Async XLA Ops:
  55.5 22.1 %all-to-all-start = ((f32[128,2,8]{2,1,0:T(2,128)}), f32[128,2,8]{2,1,0:T(2,128)S(1)}, u32[]{:S(2)}, u32[]{:S(2)}) async-start(f32[128,2,8]{2,1,0:T(2,128)} %copy.287), calls=%async_computation | async-start | bytes 262144 | tf_op jit(solution)/shard_map/all_to_all | solution.py:47
  77.5 23.4 %all-to-all-start.1 = ((bf16[128,2,8,128]{3,2,1,0:T(8,128)(2,1)}), bf16[128,2,8,128]{3,2,1,0:T(8,128)(2,1)S(1)}, u32[]{:S(2)}, u32[]{:S(2)}) async-start(bf16[128,2,8,128]{3,2,1,0:T(8,128)(2,1)} %copy.290), calls=%async_computation.1 | async-start | bytes 1048576 | tf_op jit(solution)/shard_map/all_to_all | solution.py:46
  155.2 14.7 %all-to-all-start.2 = ((f32[128,2,8]{2,1,0:T(2,128)}), f32[128,2,8]{2,1,0:T(2,128)S(1)}, u32[]{:S(2)}, u32[]{:S(2)}) async-start(f32[128,2,8]{2,1,0:T(2,128)} %copy.294), calls=%async_computation.2 | async-start | bytes 262144 | tf_op jit(solution)/shard_map/all_to_all | solution.py:47
  169.9 20.1 %all-to-all-start.3 = ((bf16[128,2,8,128]{3,2,1,0:T(8,128)(2,1)}), bf16[128,2,8,128]{3,2,1,0:T(8,128)(2,1)S(1)}, u32[]{:S(2)}, u32[]{:S(2)}) async-start(bf16[128,2,8,128]{3,2,1,0:T(8,128)(2,1)} %copy.297), calls=%async_computation.3 | async-start | bytes 1048576 | tf_op jit(solution)/shard_map/all_to_all | solution.py:46
  258.9 20.6 %all-to-all-start.5 = ((bf16[128,2,8,128]{3,2,1,0:T(8,128)(2,1)}), bf16[128,2,8,128]{3,2,1,0:T(8,128)(2,1)S(1)}, u32[]{:S(2)}, u32[]{:S(2)}) async-start(bf16[128,2,8,128]{3,2,1,0:T(8,128)(2,1)} %copy.304), calls=%async_computation.5 | async-start | bytes 1048576 | tf_op jit(solution)/shard_map/all_to_all | solution.py:46
  348.5 18.6 %all-to-all-start.7 = ((bf16[128,2,8,128]{3,2,1,0:T(8,128)(2,1)}), bf16[128,2,8,128]{3,2,1,0:T(8,128)(2,1)S(1)}, u32[]{:S(2)}, u32[]{:S(2)}) async-start(bf16[128,2,8,128]{3,2,1,0:T(8,128)(2,1)} %copy.311), calls=%async_computation.7 | async-start | bytes 1048576 | tf_op jit(solution)/shard_map/all_to_all | solution.py:46
  420.2 14.7 %all-to-all-start.8 = ((f32[128,2,8]{2,1,0:T(2,128)}), f32[128,2,8]{2,1,0:T(2,128)S(1)}, u32[]{:S(2)}, u32[]{:S(2)}) async-start(f32[128,2,8]{2,1,0:T(2,128)} %copy.315), calls=%async_computation.8 | async-start | bytes 262144 | tf_op jit(solution)/shard_map/all_to_all | solution.py:47
  434.9 17.9 %all-to-all-start.9 = ((bf16[128,2,8,128]{3,2,1,0:T(8,128)(2,1)}), bf16[128,2,8,128]{3,2,1,0:T(8,128)(2,1)S(1)}, u32[]{:S(2)}, u32[]{:S(2)}) async-start(bf16[128,2,8,128]{3,2,1,0:T(8,128)(2,1)} %copy.318), calls=%async_computation.9 | async-start | bytes 1048576 | tf_op jit(solution)/shard_map/all_to_all | solution.py:46
  504.2 14.7 %all-to-all-start.10 = ((f32[128,2,8]{2,1,0:T(2,128)}), f32[128,2,8]{2,1,0:T(2,128)S(1)}, u32[]{:S(2)}, u32[]{:S(2)}) async-start(f32[128,2,8]{2,1,0:T(2,128)} %copy.322), calls=%async_computation.10 | async-start | bytes 262144 | tf_op jit(solution)/shard_map/all_to_all | solution.py:47
  518.9 18.1 %all-to-all-start.11 = ((bf16[128,2,8,128]{3,2,1,0:T(8,128)(2,1)}), bf16[128,2,8,128]{3,2,1,0:T(8,128)(2,1)S(1)}, u32[]{:S(2)}, u32[]{:S(2)}) async-start(bf16[128,2,8,128]{3,2,1,0:T(8,128)(2,1)} %copy.325), calls=%async_computation.11 | async-start | bytes 1048576 | tf_op jit(solution)/shard_map/all_to_all | solution.py:46
  588.4 14.7 %all-to-all-start.12 = ((f32[128,2,8]{2,1,0:T(2,128)}), f32[128,2,8]{2,1,0:T(2,128)S(1)}, u32[]{:S(2)}, u32[]{:S(2)}) async-start(f32[128,2,8]{2,1,0:T(2,128)} %copy.329), calls=%async_computation.12 | async-start | bytes 262144 | tf_op jit(solution)/shard_map/all_to_all | solution.py:47
  603.1 17.8 %all-to-all-start.13 = ((bf16[128,2,8,128]{3,2,1,0:T(8,128)(2,1)}), bf16[128,2,8,128]{3,2,1,0:T(8,128)(2,1)S(1)}, u32[]{:S(2)}, u32[]{:S(2)}) async-start(bf16[128,2,8,128]{3,2,1,0:T(8,128)(2,1)} %copy.332), calls=%async_computation.13 | async-start | bytes 1048576 | tf_op jit(solution)/shard_map/all_to_all | solution.py:46
  687.0 17.9 %all-to-all-start.15 = ((bf16[128,2,8,128]{3,2,1,0:T(8,128)(2,1)}), bf16[128,2,8,128]{3,2,1,0:T(8,128)(2,1)S(1)}, u32[]{:S(2)}, u32[]{:S(2)}) async-start(bf16[128,2,8,128]{3,2,1,0:T(8,128)(2,1)} %copy.339), calls=%async_computation.15 | async-start | bytes 1048576 | tf_op jit(solution)/shard_map/all_to_all | solution.py:46
  771.0 18.1 %all-to-all-start.17 = ((bf16[128,2,8,128]{3,2,1,0:T(8,128)(2,1)}), bf16[128,2,8,128]{3,2,1,0:T(8,128)(2,1)S(1)}, u32[]{:S(2)}, u32[]{:S(2)}) async-start(bf16[128,2,8,128]{3,2,1,0:T(8,128)(2,1)} %copy.346), calls=%async_computation.17 | async-start | bytes 1048576 | tf_op jit(solution)/shard_map/all_to_all | solution.py:46
  840.5 14.7 %all-to-all-start.18 = ((f32[128,2,8]{2,1,0:T(2,128)}), f32[128,2,8]{2,1,0:T(2,128)S(1)}, u32[]{:S(2)}, u32[]{:S(2)}) async-start(f32[128,2,8]{2,1,0:T(2,128)} %copy.350), calls=%async_computation.18 | async-start | bytes 262144 | tf_op jit(solution)/shard_map/all_to_all | solution.py:47
  855.2 17.8 %all-to-all-start.19 = ((bf16[128,2,8,128]{3,2,1,0:T(8,128)(2,1)}), bf16[128,2,8,128]{3,2,1,0:T(8,128)(2,1)S(1)}, u32[]{:S(2)}, u32[]{:S(2)}) async-start(bf16[128,2,8,128]{3,2,1,0:T(8,128)(2,1)} %copy.353), calls=%async_computation.19 | async-start | bytes 1048576 | tf_op jit(solution)/shard_map/all_to_all | solution.py:46
  939.2 17.9 %all-to-all-start.21 = ((bf16[128,2,8,128]{3,2,1,0:T(8,128)(2,1)}), bf16[128,2,8,128]{3,2,1,0:T(8,128)(2,1)S(1)}, u32[]{:S(2)}, u32[]{:S(2)}) async-start(bf16[128,2,8,128]{3,2,1,0:T(8,128)(2,1)} %copy.360), calls=%async_computation.21 | async-start | bytes 1048576 | tf_op jit(solution)/shard_map/all_to_all | solution.py:46
  1023.2 18.1 %all-to-all-start.23 = ((bf16[128,2,8,128]{3,2,1,0:T(8,128)(2,1)}), bf16[128,2,8,128]{3,2,1,0:T(8,128)(2,1)S(1)}, u32[]{:S(2)}, u32[]{:S(2)}) async-start(bf16[128,2,8,128]{3,2,1,0:T(8,128)(2,1)} %copy.367), calls=%async_computation.23 | async-start | bytes 1048576 | tf_op jit(solution)/shard_map/all_to_all | solution.py:46
  1092.7 14.7 %all-to-all-start.24 = ((f32[128,2,8]{2,1,0:T(2,128)}), f32[128,2,8]{2,1,0:T(2,128)S(1)}, u32[]{:S(2)}, u32[]{:S(2)}) async-start(f32[128,2,8]{2,1,0:T(2,128)} %copy.371), calls=%async_computation.24 | async-start | bytes 262144 | tf_op jit(solution)/shard_map/all_to_all | solution.py:47
  1107.4 17.8 %all-to-all-start.25 = ((bf16[128,2,8,128]{3,2,1,0:T(8,128)(2,1)}), bf16[128,2,8,128]{3,2,1,0:T(8,128)(2,1)S(1)}, u32[]{:S(2)}, u32[]{:S(2)}) async-start(bf16[128,2,8,128]{3,2,1,0:T(8,128)(2,1)} %copy.374), calls=%async_computation.25 | async-start | bytes 1048576 | tf_op jit(solution)/shard_map/all_to_all | solution.py:46
  1191.4 17.9 %all-to-all-start.27 = ((bf16[128,2,8,128]{3,2,1,0:T(8,128)(2,1)}), bf16[128,2,8,128]{3,2,1,0:T(8,128)(2,1)S(1)}, u32[]{:S(2)}, u32[]{:S(2)}) async-start(bf16[128,2,8,128]{3,2,1,0:T(8,128)(2,1)} %copy.381), calls=%async_computation.27 | async-start | bytes 1048576 | tf_op jit(solution)/shard_map/all_to_all | solution.py:46
  1260.8 14.7 %all-to-all-start.28 = ((f32[128,2,8]{2,1,0:T(2,128)}), f32[128,2,8]{2,1,0:T(2,128)S(1)}, u32[]{:S(2)}, u32[]{:S(2)}) async-start(f32[128,2,8]{2,1,0:T(2,128)} %copy.385), calls=%async_computation.28 | async-start | bytes 262144 | tf_op jit(solution)/shard_map/all_to_all | solution.py:47
  1275.5 17.9 %all-to-all-start.29 = ((bf16[128,2,8,128]{3,2,1,0:T(8,128)(2,1)}), bf16[128,2,8,128]{3,2,1,0:T(8,128)(2,1)S(1)}, u32[]{:S(2)}, u32[]{:S(2)}) async-start(bf16[128,2,8,128]{3,2,1,0:T(8,128)(2,1)} %copy.388), calls=%async_computation.29 | async-start | bytes 1048576 | tf_op jit(solution)/shard_map/all_to_all | solution.py:46
  1359.7 17.6 %all-to-all-start.31 = ((bf16[128,2,8,128]{3,2,1,0:T(8,128)(2,1)}), bf16[128,2,8,128]{3,2,1,0:T(8,128)(2,1)S(1)}, u32[]{:S(2)}, u32[]{:S(2)}) async-start(bf16[128,2,8,128]{3,2,1,0:T(8,128)(2,1)} %copy.395), calls=%async_computation.31 | async-start | bytes 1048576 | tf_op jit(solution)/shard_map/all_to_all | solution.py:46
  (48 other events, 561.7 us)
where the time goes:
time: 1400 us; the launch traced here: 1380 us
  blocking collectives  557 us (40%)
  waiting for transfers between devices  295 us (21%)
  matrix products  246 us (18%)
  starting transfers between devices  159 us (11%)
  other arithmetic  78.1 us (6%)
  local copies, waits for them, and re-layouts  45.6 us (3%)
    all_gather x16, blocking collectives, local_step(): group_queries = lax.all_gather(queries, 'ctx', axis=0, tiled=True)  557 us
    all_to_all x16, waiting for transfers between devices, local_step(): lax.all_to_all(part_out, 'ctx', 0, 0, tiled=True)  191 us
    all_to_all x16, waiting for transfers between devices, local_step(): lax.all_to_all(part_lse, 'ctx', 0, 0, tiled=True)  104 us
    all_to_all x16, starting transfers between devices, local_step(): lax.all_to_all(part_out, 'ctx', 0, 0, tiled=True)  84 us
    all_to_all x16, starting transfers between devices, local_step(): lax.all_to_all(part_lse, 'ctx', 0, 0, tiled=True)  74.8 us
    dot_general x16, matrix products, local_step(): jnp.dot(hidden, w_query[layer_idx], preferred_element_type=jnp.float32)  73.4 us
    dot_general x16, matrix products, local_step(): jnp.dot(attended, w_out[layer_idx], preferred_element_type=jnp.float32)  73.2 us
  transfers between devices with their start and end apart: 32, of which 31 were waited for; matrix products, arithmetic and copies ran while one was open for 6% of the time, Pallas kernels for 0%

commit v1 on v0

--- a/solution.py
+++ b/solution.py
@@ -1,7 +1,87 @@
+import functools
+
 import jax
 import jax.numpy as jnp
 from jax import lax
+from jax.experimental import pallas as pl
+from jax.experimental.pallas import tpu as pltpu
 from jax.sharding import PartitionSpec as P
+
+
+MESH = pl.DeviceIdType.MESH
+
+
+def enter(me, count):
+    barrier = pltpu.get_barrier_semaphore()
+
+    def greet(step, carry):
+        pl.semaphore_signal(barrier, inc=1, device_id={'ctx': (me + step) % count}, device_id_type=MESH)
+        return carry
+
+    lax.fori_loop(1, count, greet, 0)
+    pl.semaphore_wait(barrier, count - 1)
+
+
+def spread_body(count, row_ref, all_ref, send_sem, recv_sem):
+    me = lax.axis_index('ctx')
+    enter(me, count)
+
+    def push(step, carry):
+        pltpu.make_async_remote_copy(
+            src_ref=row_ref.at[0], dst_ref=all_ref.at[me], send_sem=send_sem, recv_sem=recv_sem,
+            device_id={'ctx': (me + step) % count}, device_id_type=MESH).start()
+        return carry
+
+    lax.fori_loop(1, count, push, 0)
+    all_ref[me] = row_ref[0]
+    others = all_ref.at[pl.ds(0, count - 1)]
+    pltpu.make_async_copy(others, others, send_sem).wait()
+    pltpu.make_async_copy(others, others, recv_sem).wait()
+
+
+def swap_body(count, val_ref, lse_ref, vals_ref, lses_ref, send_sem, recv_sem, send_lse, recv_lse):
+    me = lax.axis_index('ctx')
+    enter(me, count)
+
+    def push(step, carry):
+        target = (me + step) % count
+        pltpu.make_async_remote_copy(
+            src_ref=val_ref.at[target], dst_ref=vals_ref.at[me], send_sem=send_sem, recv_sem=recv_sem,
+            device_id={'ctx': target}, device_id_type=MESH).start()
+        pltpu.make_async_remote_copy(
+            src_ref=lse_ref.at[target], dst_ref=lses_ref.at[me], send_sem=send_lse, recv_sem=recv_lse,
+            device_id={'ctx': target}, device_id_type=MESH).start()
+        return carry
+
+    lax.fori_loop(1, count, push, 0)
+    vals_ref[me] = val_ref[me]
+    lses_ref[me] = lse_ref[me]
+    for block, out_sem, in_sem in ((vals_ref, send_sem, recv_sem), (lses_ref, send_lse, recv_lse)):
+        others = block.at[pl.ds(0, count - 1)]
+        pltpu.make_async_copy(others, others, out_sem).wait()
+        pltpu.make_async_copy(others, others, in_sem).wait()
+
+
+def spread(count, row):
+    vmem = pl.BlockSpec(memory_space=pltpu.VMEM)
+    return pl.pallas_call(
+        functools.partial(spread_body, count),
+        out_shape=jax.ShapeDtypeStruct((count,) + row.shape[1:], row.dtype),
+        in_specs=[vmem], out_specs=vmem,
+        scratch_shapes=[pltpu.SemaphoreType.DMA, pltpu.SemaphoreType.DMA],
+        compiler_params=pltpu.CompilerParams(collective_id=0, has_side_effects=True),
+    )(row)
+
+
+def swap(count, val, lse):
+    vmem = pl.BlockSpec(memory_space=pltpu.VMEM)
+    return pl.pallas_call(
+        functools.partial(swap_body, count),
+        out_shape=(jax.ShapeDtypeStruct(val.shape, val.dtype), jax.ShapeDtypeStruct(lse.shape, lse.dtype)),
+        in_specs=[vmem, vmem], out_specs=(vmem, vmem),
+        scratch_shapes=[pltpu.SemaphoreType.DMA] * 4,
+        compiler_params=pltpu.CompilerParams(collective_id=1, has_side_effects=True),
+    )(val, lse)
 
 
 def solution(mesh):
@@ -35,7 +115,7 @@
             v_cache = jnp.where(slot_hit, v_new, v_suffix[layer_idx])
             k_layers.append(k_cache)
             v_layers.append(v_cache)
-            group_queries = lax.all_gather(queries, 'ctx', axis=0, tiled=True)
+            group_queries = spread(ctx_size, queries.reshape(home_rows, num_heads, head_dim)).reshape(ctx_size, kv_heads, group_size, head_dim)
             pre_scores = jnp.einsum('bkgd,pkd->bkgp', group_queries, k_prefix[layer_idx], preferred_element_type=jnp.float32) * score_scale
             pre_max = pre_scores.max(axis=-1)
             pre_exp = jnp.exp(pre_scores - pre_max[..., None])
@@ -43,8 +123,10 @@
             pre_vals = jnp.einsum('bkgp,pkd->bkgd', pre_exp.astype(jnp.bfloat16), v_prefix[layer_idx], preferred_element_type=jnp.float32)
             part_out = (pre_vals / pre_mass[..., None]).astype(jnp.bfloat16)
             part_lse = pre_max + jnp.log(pre_mass)
-            home_out = lax.all_to_all(part_out, 'ctx', 0, 0, tiled=True).reshape(ctx_size, home_rows, kv_heads, group_size, head_dim)
-            home_lse = lax.all_to_all(part_lse, 'ctx', 0, 0, tiled=True).reshape(ctx_size, home_rows, kv_heads, group_size)
+            wide_lse = jnp.pad(part_lse.reshape(ctx_size, 1, num_heads), ((0, 0), (0, 0), (0, head_dim - num_heads)))
+            home_out, home_lse = swap(ctx_size, part_out.reshape(ctx_size, num_heads, head_dim), wide_lse)
+            home_out = home_out.reshape(ctx_size, home_rows, kv_heads, group_size, head_dim)
+            home_lse = home_lse[:, 0, :num_heads].reshape(ctx_size, home_rows, kv_heads, group_size)
             suf_scores = jnp.einsum('bkgd,bskd->bkgs', queries, k_cache, preferred_element_type=jnp.float32) * score_scale
             suf_scores = jnp.where(slot_live, suf_scores, -jnp.inf)
             suf_max = suf_scores.max(axis=-1)

time: 1400 us -> 1080 us (0.77)
  Pallas kernels: 0 us -> 563 us
  blocking collectives: 557 us -> 0 us
  waiting for transfers between devices: 295 us -> 0 us
  starting transfers between devices: 159 us -> 0 us
  other arithmetic: 78.1 us -> 142 us
  matrix products: 246 us -> 300 us
    pallas_call x0 -> x32, Pallas kernels: none -> 563 us  [the longest x16 295 us: swap(): pl.pallas_call(functools.partial(swap_body, count), out_shape=(jax.ShapeD...]
    all_gather x16 -> x0, blocking collectives: 557 us -> none  [local_step(): group_queries = lax.all_gather(queries, 'ctx', axis=0, tiled=True)]
    all_to_all x32 -> x0, waiting for transfers between devices: 295 us -> none  [the longest x16 191 us: local_step(): lax.all_to_all(part_out, 'ctx', 0, 0, tiled=True)]
    all_to_all x32 -> x0, starting transfers between devices: 159 us -> none  [the longest x16 84 us: local_step(): lax.all_to_all(part_out, 'ctx', 0, 0, tiled=True)]
    dot_general x16, matrix products: 12.6 us -> 50.3 us  [local_step(): jnp.einsum('bkgd,pkd->bkgp', group_queries, k_prefix[layer_idx], preferre...]
    dot_general x16, matrix products: 21.6 us -> 49.5 us  [local_step(): jnp.einsum('bkgp,pkd->bkgd', pre_exp.astype(jnp.bfloat16), v_prefix[layer...]
    reduce_sum x16, other arithmetic: 20.9 us -> 41.8 us  [local_step(): pre_mass = pre_exp.sum(axis=-1)]
  transfers between devices with their start and end apart: 32 -> 0, of which waited for: 31 -> 0; matrix products, arithmetic and copies ran while one was open for 6% -> 0% of each run, Pallas kernels for 0% -> 0%
where the time goes in v1:
time: 1080 us; the launch traced here: 1060 us
  Pallas kernels  563 us (52%)
  matrix products  300 us (28%)
  other arithmetic  142 us (13%)
  local copies, waits for them, and re-layouts  53.6 us (5%)
    pallas_call x16, Pallas kernels, swap(): pl.pallas_call(functools.partial(swap_body, count), out_shape=(jax.ShapeD...  295 us
    pallas_call x16, Pallas kernels, spread(): pl.pallas_call(functools.partial(spread_body, count), out_shape=jax.Shape...  267 us
    dot_general x16, matrix products, local_step(): jnp.dot(hidden, w_query[layer_idx], preferred_element_type=jnp.float32)  73.3 us
    dot_general x16, matrix products, local_step(): jnp.dot(attended, w_out[layer_idx], preferred_element_type=jnp.float32)  73.2 us
    dot_general x16, matrix products, local_step(): jnp.einsum('bkgd,pkd->bkgp', group_queries, k_prefix[layer_idx], preferre...  50.3 us
    dot_general x16, matrix products, local_step(): jnp.einsum('bkgp,pkd->bkgd', pre_exp.astype(jnp.bfloat16), v_prefix[layer...  49.5 us
    reduce_sum x16, other arithmetic, local_step(): pre_mass = pre_exp.sum(axis=-1)  41.8 us
    dot_general x16, matrix products, local_step(): jnp.dot(hidden, w_value[layer_idx], preferred_element_type=jnp.float32)  23.5 us

profile of v1, /device:TPU:1, one launch (start us, length us, event | category | flops | bytes accessed | tf_op | source)
XLA Modules:
  0.0 1061.5 jit_solution(8134425061332948520)
XLA Ops:
  12.0 21.1 %shard_map.121 = bf16[128,16,128]{2,1,0:T(8,128)(2,1)} custom-call(bf16[1,16,128]{2,1,0:T(8,128)(2,1)} %convert_bitcast_fusion.15.row_ref), custom_call_target="tpu_custom_call" | custom-call | tf_op jit(solution)/shard_map/pallas_call | solution.py:67
  44.1 18.6 %shard_map.122 = (bf16[128,16,128]{2,1,0:T(8,128)(2,1)}, f32[128,1,128]{2,1,0:T(1,128)}) custom-call(bf16[128,16,128]{2,1,0:T(8,128)(2,1)} %bitcast.1410, f32[128,1,128]{2,1,0:T(1,128)} %pad.49.lse_ref), custom_call_target="tpu_custom_call" | custom-call | tf_op jit(solution)/shard_map/pallas_call | solution.py:78
  112.2 18.3 %shard_map.124 = (bf16[128,16,128]{2,1,0:T(8,128)(2,1)}, f32[128,1,128]{2,1,0:T(1,128)}) custom-call(bf16[128,16,128]{2,1,0:T(8,128)(2,1)} %bitcast.1411, f32[128,1,128]{2,1,0:T(1,128)} %pad.50.lse_ref), custom_call_target="tpu_custom_call" | custom-call | tf_op jit(solution)/shard_map/pallas_call | solution.py:78
  149.8 16.4 %shard_map.125 = bf16[128,16,128]{2,1,0:T(8,128)(2,1)} custom-call(bf16[1,16,128]{2,1,0:T(8,128)(2,1)} %convert_bitcast_fusion.13.row_ref), custom_call_target="tpu_custom_call" | custom-call | tf_op jit(solution)/shard_map/pallas_call | solution.py:67
  176.4 18.3 %shard_map.126 = (bf16[128,16,128]{2,1,0:T(8,128)(2,1)}, f32[128,1,128]{2,1,0:T(1,128)}) custom-call(bf16[128,16,128]{2,1,0:T(8,128)(2,1)} %bitcast.1412, f32[128,1,128]{2,1,0:T(1,128)} %pad.51.lse_ref), custom_call_target="tpu_custom_call" | custom-call | tf_op jit(solution)/shard_map/pallas_call | solution.py:78
  214.0 16.8 %shard_map.127 = bf16[128,16,128]{2,1,0:T(8,128)(2,1)} custom-call(bf16[1,16,128]{2,1,0:T(8,128)(2,1)} %convert_bitcast_fusion.12.row_ref), custom_call_target="tpu_custom_call" | custom-call | tf_op jit(solution)/shard_map/pallas_call | solution.py:67
  242.8 17.8 %shard_map.128 = (bf16[128,16,128]{2,1,0:T(8,128)(2,1)}, f32[128,1,128]{2,1,0:T(1,128)}) custom-call(bf16[128,16,128]{2,1,0:T(8,128)(2,1)} %bitcast.1413, f32[128,1,128]{2,1,0:T(1,128)} %pad.52.lse_ref), custom_call_target="tpu_custom_call" | custom-call | tf_op jit(solution)/shard_map/pallas_call | solution.py:78
  279.9 16.9 %shard_map.129 = bf16[128,16,128]{2,1,0:T(8,128)(2,1)} custom-call(bf16[1,16,128]{2,1,0:T(8,128)(2,1)} %convert_bitcast_fusion.11.row_ref), custom_call_target="tpu_custom_call" | custom-call | tf_op jit(solution)/shard_map/pallas_call | solution.py:67
  308.9 17.9 %shard_map.130 = (bf16[128,16,128]{2,1,0:T(8,128)(2,1)}, f32[128,1,128]{2,1,0:T(1,128)}) custom-call(bf16[128,16,128]{2,1,0:T(8,128)(2,1)} %bitcast.1414, f32[128,1,128]{2,1,0:T(1,128)} %pad.53.lse_ref), custom_call_target="tpu_custom_call" | custom-call | tf_op jit(solution)/shard_map/pallas_call | solution.py:78
  346.1 16.9 %shard_map.131 = bf16[128,16,128]{2,1,0:T(8,128)(2,1)} custom-call(bf16[1,16,128]{2,1,0:T(8,128)(2,1)} %convert_bitcast_fusion.10.row_ref), custom_call_target="tpu_custom_call" | custom-call | tf_op jit(solution)/shard_map/pallas_call | solution.py:67
  375.1 18.5 %shard_map.132 = (bf16[128,16,128]{2,1,0:T(8,128)(2,1)}, f32[128,1,128]{2,1,0:T(1,128)}) custom-call(bf16[128,16,128]{2,1,0:T(8,128)(2,1)} %bitcast.1415, f32[128,1,128]{2,1,0:T(1,128)} %pad.54.lse_ref), custom_call_target="tpu_custom_call" | custom-call | tf_op jit(solution)/shard_map/pallas_call | solution.py:78
  441.1 18.8 %shard_map.134 = (bf16[128,16,128]{2,1,0:T(8,128)(2,1)}, f32[128,1,128]{2,1,0:T(1,128)}) custom-call(bf16[128,16,128]{2,1,0:T(8,128)(2,1)} %bitcast.1416, f32[128,1,128]{2,1,0:T(1,128)} %pad.55.lse_ref), custom_call_target="tpu_custom_call" | custom-call | tf_op jit(solution)/shard_map/pallas_call | solution.py:78
  507.2 18.6 %shard_map.136 = (bf16[128,16,128]{2,1,0:T(8,128)(2,1)}, f32[128,1,128]{2,1,0:T(1,128)}) custom-call(bf16[128,16,128]{2,1,0:T(8,128)(2,1)} %bitcast.1417, f32[128,1,128]{2,1,0:T(1,128)} %pad.56.lse_ref), custom_call_target="tpu_custom_call" | custom-call | tf_op jit(solution)/shard_map/pallas_call | solution.py:78
  545.0 16.6 %shard_map.137 = bf16[128,16,128]{2,1,0:T(8,128)(2,1)} custom-call(bf16[1,16,128]{2,1,0:T(8,128)(2,1)} %convert_bitcast_fusion.7.row_ref), custom_call_target="tpu_custom_call" | custom-call | tf_op jit(solution)/shard_map/pallas_call | solution.py:67
  573.8 18.3 %shard_map.138 = (bf16[128,16,128]{2,1,0:T(8,128)(2,1)}, f32[128,1,128]{2,1,0:T(1,128)}) custom-call(bf16[128,16,128]{2,1,0:T(8,128)(2,1)} %bitcast.1418, f32[128,1,128]{2,1,0:T(1,128)} %pad.57.lse_ref), custom_call_target="tpu_custom_call" | custom-call | tf_op jit(solution)/shard_map/pallas_call | solution.py:78
  639.8 18.4 %shard_map.140 = (bf16[128,16,128]{2,1,0:T(8,128)(2,1)}, f32[128,1,128]{2,1,0:T(1,128)}) custom-call(bf16[128,16,128]{2,1,0:T(8,128)(2,1)} %bitcast.1419, f32[128,1,128]{2,1,0:T(1,128)} %pad.58.lse_ref), custom_call_target="tpu_custom_call" | custom-call | tf_op jit(solution)/shard_map/pallas_call | solution.py:78
  677.5 17.4 %shard_map.141 = bf16[128,16,128]{2,1,0:T(8,128)(2,1)} custom-call(bf16[1,16,128]{2,1,0:T(8,128)(2,1)} %convert_bitcast_fusion.5.row_ref), custom_call_target="tpu_custom_call" | custom-call | tf_op jit(solution)/shard_map/pallas_call | solution.py:67
  707.1 17.8 %shard_map.142 = (bf16[128,16,128]{2,1,0:T(8,128)(2,1)}, f32[128,1,128]{2,1,0:T(1,128)}) custom-call(bf16[128,16,128]{2,1,0:T(8,128)(2,1)} %bitcast.1420, f32[128,1,128]{2,1,0:T(1,128)} %pad.59.lse_ref), custom_call_target="tpu_custom_call" | custom-call | tf_op jit(solution)/shard_map/pallas_call | solution.py:78
  772.3 18.9 %shard_map.144 = (bf16[128,16,128]{2,1,0:T(8,128)(2,1)}, f32[128,1,128]{2,1,0:T(1,128)}) custom-call(bf16[128,16,128]{2,1,0:T(8,128)(2,1)} %bitcast.1421, f32[128,1,128]{2,1,0:T(1,128)} %pad.60.lse_ref), custom_call_target="tpu_custom_call" | custom-call | tf_op jit(solution)/shard_map/pallas_call | solution.py:78
  838.7 18.7 %shard_map.146 = (bf16[128,16,128]{2,1,0:T(8,128)(2,1)}, f32[128,1,128]{2,1,0:T(1,128)}) custom-call(bf16[128,16,128]{2,1,0:T(8,128)(2,1)} %bitcast.1422, f32[128,1,128]{2,1,0:T(1,128)} %pad.61.lse_ref), custom_call_target="tpu_custom_call" | custom-call | tf_op jit(solution)/shard_map/pallas_call | solution.py:78
  876.8 16.4 %shard_map.147 = bf16[128,16,128]{2,1,0:T(8,128)(2,1)} custom-call(bf16[1,16,128]{2,1,0:T(8,128)(2,1)} %convert_bitcast_fusion.2.row_ref), custom_call_target="tpu_custom_call" | custom-call | tf_op jit(solution)/shard_map/pallas_call | solution.py:67
  905.2 18.5 %shard_map.148 = (bf16[128,16,128]{2,1,0:T(8,128)(2,1)}, f32[128,1,128]{2,1,0:T(1,128)}) custom-call(bf16[128,16,128]{2,1,0:T(8,128)(2,1)} %bitcast.1423, f32[128,1,128]{2,1,0:T(1,128)} %pad.62.lse_ref), custom_call_target="tpu_custom_call" | custom-call | tf_op jit(solution)/shard_map/pallas_call | solution.py:78
  968.1 19.5 %shard_map.150 = (bf16[128,16,128]{2,1,0:T(8,128)(2,1)}, f32[128,1,128]{2,1,0:T(1,128)}) custom-call(bf16[128,16,128]{2,1,0:T(8,128)(2,1)} %bitcast.1424, f32[128,1,128]{2,1,0:T(1,128)} %pad.63.lse_ref), custom_call_target="tpu_custom_call" | custom-call | tf_op jit(solution)/shard_map/pallas_call | solution.py:78
  1033.4 18.6 %shard_map.152 = (bf16[128,16,128]{2,1,0:T(8,128)(2,1)}, f32[128,1,128]{2,1,0:T(1,128)}) custom-call(bf16[128,16,128]{2,1,0:T(8,128)(2,1)} %bitcast.1425, f32[128,1,128]{2,1,0:T(1,128)} %pad.64.lse_ref), custom_call_target="tpu_custom_call" | custom-call | tf_op jit(solution)/shard_map/pallas_call | solution.py:78
  (582 shorter events, 624.4 us)
Async XLA Ops:
  0.6 6.2 copy-start.24
  40.8 26.5 %copy-start.8 = (bf16[16,1,32,2,128]{4,3,2,1,0:T(2,128)(2,1)S(1)}, bf16[16,1,32,2,128]{4,3,2,1,0:T(2,128)(2,1)}, u32[]{:S(2)}) copy-start(bf16[16,1,32,2,128]{4,3,2,1,0:T(2,128)(2,1)} %param.18) | copy-start | bytes 786436
  79.0 5.4 copy-start.27
  107.8 23.6 %copy-start.30 = (f32[16]{0:T(128)S(1)}, f32[16]{0:T(128)}, u32[]{:S(2)}) copy-start(f32[16]{0:T(128)} %reduce_max.504) | copy-start | bytes 196
  134.3 6.1 copy-start.9
  168.0 4.0 copy-start.22
  296.8 7.8 copy-start.21
  363.0 7.7 copy-start.20
  429.0 7.8 copy-start.19
  495.1 7.8 copy-start.18
  561.7 7.8 copy-start.17
  627.7 7.8 copy-start.16
  695.0 7.8 copy-start.15
  760.2 7.8 copy-start.14
  826.7 7.8 copy-start.13
  861.1 32.1 %copy-start.7 = (bf16[1,512,2,128]{3,2,1,0:T(2,128)(2,1)S(1)}, bf16[1,512,2,128]{3,2,1,0:T(2,128)(2,1)}, u32[]{:S(2)}) copy-start(bf16[1,512,2,128]{3,2,1,0:T(2,128)(2,1)} %get-tuple-element.117) | copy-start | bytes 786436
  893.1 7.7 copy-start.12
  927.5 6.1 copy-start.26
  935.9 21.9 %copy-start.6 = (bf16[1,512,2,128]{3,2,1,0:T(2,128)(2,1)S(1)}, bf16[1,512,2,128]{3,2,1,0:T(2,128)(2,1)}, u32[]{:S(2)}) copy-start(bf16[1,512,2,128]{3,2,1,0:T(2,128)(2,1)} %get-tuple-element.116) | copy-start | bytes 786436
  957.8 5.9 copy-start.11
  991.4 6.1 copy-start.28
  1001.3 4.8 copy-start.29
  1001.4 21.7 %copy-start.5 = (bf16[1,512,2,128]{3,2,1,0:T(2,128)(2,1)S(1)}, bf16[1,512,2,128]{3,2,1,0:T(2,128)(2,1)}, u32[]{:S(2)}) copy-start(bf16[1,512,2,128]{3,2,1,0:T(2,128)(2,1)} %get-tuple-element.115) | copy-start | bytes 786436
  1023.2 5.9 copy-start.10
  (7 other events, 15.9 us)
